TPU v7x, 32 devices: a 4x4x1 block of a 4x4x8 slice. The times are simulated.
32 devices in a mesh: dp: 1 (over z), tp: 32 (over y, x, core).
Axes of the slice: x: 4, y: 4, z: 1, core: 2. Of those that a mesh axis runs over, the one named last changes fastest.
The devices are a block of a 4x4x8 slice.
Arguments:
- hidden: bfloat16 [4096, 2048], P(('dp', 'tp'))
- w_head: bfloat16 [2048, 128256], P(None, 'tp')
- labels: int32 [4096], P(('dp', 'tp'))
Outputs:
- output 1: float32 [1], P('dp')
- output 2: bfloat16 [4096, 2048], P(('dp', 'tp'))
- output 3: bfloat16 [2048, 128256], P('dp', 'tp')
All inputs are finite; a program needn't handle non-finite values.
Results may differ from a plain program's by a relative error of at most 0.001.
Values are sent between devices in bfloat16 or wider.
A program may use at most 768 MiB of HBM per device.

v0:
```python
import jax
import jax.numpy as jnp
from jax import lax
from jax.sharding import PartitionSpec as P


def solution(mesh):
    group_size = mesh.shape["tp"]

    def local_step(hid_loc, w_loc, lab_loc):
        inv_tokens = 1.0 / (hid_loc.shape[0] * group_size)
        vocab_loc = w_loc.shape[1]
        hid_all = lax.all_gather(hid_loc, "tp", axis=0, tiled=True)
        lab_all = lax.all_gather(lab_loc, "tp", axis=0, tiled=True)
        logits = jnp.dot(hid_all, w_loc, preferred_element_type=jnp.float32)
        glob_max = lax.pmax(jnp.max(logits, axis=1), "tp")
        shifted = jnp.exp(logits - glob_max[:, None])
        local_ids = lab_all - lax.axis_index("tp") * vocab_loc
        is_label = jnp.arange(vocab_loc, dtype=jnp.int32) == local_ids[:, None]
        local_stats = jnp.stack([jnp.sum(shifted, axis=1), jnp.sum(jnp.where(is_label, logits, 0.0), axis=1)])
        stat_sums = lax.psum(local_stats, "tp")
        row_sum = stat_sums[0]
        token_loss = glob_max + jnp.log(row_sum) - stat_sums[1]
        mean_loss = (jnp.sum(token_loss) * inv_tokens).reshape(1)
        prob_rows = shifted / row_sum[:, None]
        grad_out = (jnp.where(is_label, prob_rows - 1.0, prob_rows) * inv_tokens).astype(jnp.bfloat16)
        d_head = lax.dot_general(hid_all, grad_out, (((0,), (0,)), ((), ())), preferred_element_type=jnp.float32)
        dx_part = lax.dot_general(grad_out, w_loc, (((1,), (1,)), ((), ())), preferred_element_type=jnp.float32)
        d_hidden = lax.psum_scatter(dx_part, "tp", scatter_dimension=0, tiled=True)
        return mean_loss, d_hidden.astype(jnp.bfloat16), d_head.astype(jnp.bfloat16)

    return jax.shard_map(
        local_step,
        mesh=mesh,
        in_specs=(P(("dp", "tp"), None), P(None, "tp"), P(("dp", "tp"))),
        out_specs=(P("dp"), P(("dp", "tp"), None), P("dp", "tp")),
        check_vma=False,
    )
```

profile of v0, /device:TPU:97, one launch (start us, length us, event | category | flops | bytes accessed | tf_op | source)
XLA Modules:
  0.0 549.8 jit_solution(7030516822142224739)
XLA Ops:
  7.2 0.1 all-gather.3.cloned.1.call-start
  7.2 0.7 all-gather.3.cloned.1.call-update
  8.0 0.1 reduce-scatter.2.cloned.1.call-start
  8.0 32.2 %all-gather = s32[32,1,128]{2,1,0:T(1,128)S(1)} all-gather(s32[1,1,128]{2,1,0:T(1,128)} %bitcast.25), channel_id=1, replica_groups=mesh['dp'=1,'tp'=32] {'tp'}, dimensions={0}, use_global_device_ids=true | all-gather | bytes 16896 | tf_op jit(solution)/shard_map/all_gather | solution.py:14
  40.2 0.6 broadcast_subtract_fusion
  40.8 40.8 %all-gather.3.cloned.1.call-done = bf16[4096,2048]{1,0:T(8,128)(2,1)} async-done(((bf16[128,2048]{1,0:T(8,128)(2,1)}), bf16[4096,2048]{1,0:T(8,128)(2,1)}) %all-gather.3.cloned.1.call-update) | async-done | bytes 16777232 | tf_op jit(solution)/shard_map/all_gather | solution.py:13
  81.7 0.0 copy-start
  81.7 78.6 %fusion.4 = (f32[4096]{0:T(1024)S(1)}, f32[4096,4008]{0,1:T(8,128)}) fusion(bf16[4096,2048]{1,0:T(8,128)(2,1)} %all-gather.3.cloned.1.call-done, bf16[2048,4008]{0,1:T(8,128)(2,1)} %param.4), kind=kOutput, calls=%fused_computation.12 | convolution fusion | flops 67259494400 | bytes 98877440 | tf_op jit(solution)/shard_map/dot_general | solution.py:15
  160.3 44.9 %pmax.7 = f32[4096]{0:T(1024)S(1)} all-reduce(f32[4096]{0:T(1024)S(1)} %get-tuple-element.7), channel_id=1, replica_groups=mesh['dp'=1,'tp'=32] {'tp'}, use_global_device_ids=true, to_apply=%region_1.0 | all-reduce | flops 4096 | bytes 32768 | tf_op jit(solution)/shard_map/pmax | solution.py:16
  205.2 0.0 copy-done
  205.2 21.3 %fusion.2 = (f32[4096]{0:T(1024)S(1)}, f32[4096]{0:T(1024)S(1)}) fusion(f32[4096,4008]{0,1:T(8,128)} %get-tuple-element.8, f32[4096]{0:T(1024)S(1)} %pmax.7, s32[4096]{0:T(1024)S(1)} %bitcast.17), kind=kLoop, calls=%fused_computation.6 | loop fusion | flops 82075648 | bytes 65732608 | tf_op jit(solution)/shard_map/reduce_sum | solution.py:20
  226.6 44.7 %psum.7 = f32[2,4096]{1,0:T(2,128)S(1)} all-reduce(f32[2,4096]{1,0:T(2,128)S(1)} %pad_maximum_fusion), channel_id=1, replica_groups=mesh['dp'=1,'tp'=32] {'tp'}, use_global_device_ids=true, to_apply=%region_4.5 | all-reduce | flops 8192 | bytes 65536 | tf_op jit(solution)/shard_map/psum | solution.py:21
  271.3 33.2 %fusion.1 = bf16[4096,4008]{0,1:T(8,128)(2,1)} fusion(f32[4096,4008]{0,1:T(8,128)} %get-tuple-element.8, f32[4096]{0:T(1024)S(1)} %bitcast.19, s32[4096]{0:T(1024)S(1)} %bitcast.18, f32[4096]{0:T(1024)S(1)} %pmax.7), kind=kLoop, calls=%fused_computation.2 | loop fusion | flops 114917376 | bytes 98549760 | tf_op jit(solution)/shard_map/convert_element_type | solution.py:26
  304.5 80.6 %fusion.5 = f32[4096,2048]{1,0:T(8,128)} fusion(bf16[4096,4008]{0,1:T(8,128)(2,1)} %fusion.1, bf16[2048,4008]{0,1:T(8,128)(2,1)} %param.4), kind=kOutput, calls=%fused_computation.13 | convolution fusion | flops 67243081728 | bytes 82804736 | tf_op jit(solution)/shard_map/dot_general | solution.py:28
  385.1 0.1 reduce-scatter.2.cloned.1.call-update
  385.2 0.6 subtract_reduce_fusion
  386.5 77.7 %convert_bitcast_fusion = bf16[2048,4008]{0,1:T(8,128)(2,1)} fusion(bf16[4096,4008]{0,1:T(8,128)(2,1)} %fusion.1, bf16[4096,2048]{1,0:T(8,128)(2,1)} %all-gather.3.cloned.1.call-done), kind=kOutput, calls=%fused_computation.7 | convolution fusion | flops 67251290112 | bytes 66027520 | tf_op jit(solution)/shard_map/dot_general | solution.py:27
  464.2 75.6 %reduce-scatter.2.cloned.1.call-done = f32[128,2048]{1,0:T(8,128)} async-done(((f32[4096,2048]{1,0:T(8,128)}), f32[128,2048]{1,0:T(8,128)}) %reduce-scatter.2.cloned.1.call-update) | async-done | bytes 1048592 | tf_op jit(solution)/shard_map/reduce_scatter | solution.py:29
  539.8 2.1 convert_element_type.13
  (2 shorter events, 0.1 us)
Async XLA Ops:
  7.2 74.5 %all-gather.3.cloned.1.call-start = ((), (), s32[]{:S(2)}) async-start(), calls=%async_computation.1 | async-start | bytes 17301504 | tf_op jit(solution)/shard_map/all_gather | solution.py:13
  8.0 531.8 %reduce-scatter.2.cloned.1.call-start = ((), (), s32[]{:S(2)}) async-start(), calls=%async_computation.2 | async-start | bytes 34603008 | tf_op jit(solution)/shard_map/reduce_scatter | solution.py:29
  81.7 123.5 %copy-start = (s32[4,8,128]{2,1,0:T(8,128)S(1)}, s32[4,8,128]{2,1,0:T(8,128)}, u32[]{:S(2)}) copy-start(s32[4,8,128]{2,1,0:T(8,128)} %broadcast_subtract_fusion) | copy-start | bytes 49156
Sparse Core Ops, SparseCore 0:
  10.1 71.5 all-gather.2
  385.3 154.3 reduce-scatter.1
where the time goes:
time: 550 us
  matrix products  237 us (43%)
  blocking collectives  122 us (22%)
  waiting for transfers between devices  117 us (21%)
  other arithmetic  57.9 us (11%)
  between operations  15.9 us (3%)
    dot_general x1, matrix products, local_step(): lax.dot_general(grad_out, w_loc, (((1,), (1,)), ((), ())), preferred_elem...  80.6 us
    dot_general x1, matrix products, local_step(): logits = jnp.dot(hid_all, w_loc, preferred_element_type=jnp.float32)  78.6 us
    dot_general x1, matrix products, local_step(): lax.dot_general(hid_all, grad_out, (((0,), (0,)), ((), ())), preferred_el...  77.7 us
    reduce_scatter x1, waiting for transfers between devices, local_step(): d_hidden = lax.psum_scatter(dx_part, 'tp', scatter_dimension=0, tiled=True)  75.6 us
    pmax x1, blocking collectives, local_step(): glob_max = lax.pmax(jnp.max(logits, axis=1), 'tp')  44.9 us
    psum x1, blocking collectives, local_step(): stat_sums = lax.psum(local_stats, 'tp')  44.7 us
    all_gather x1, waiting for transfers between devices, local_step(): hid_all = lax.all_gather(hid_loc, 'tp', axis=0, tiled=True)  40.8 us
    convert_element_type x1, other arithmetic, local_step(): (jnp.where(is_label, prob_rows - 1.0, prob_rows) * inv_tokens).astype(jnp...  33.2 us
  transfers between devices with their start and end apart: 2, of which 2 were waited for; matrix products, arithmetic and copies ran while one was open for 14% of the time, Pallas kernels for 0%

commit v1 on v0

v1 whole, which is shorter than its diff:
```python
import functools
import math

import jax
import jax.numpy as jnp
from jax import lax
from jax.experimental import pallas as pl
from jax.experimental.pallas import tpu as pltpu
from jax.sharding import PartitionSpec as P

MESH = pl.DeviceIdType.MESH
LANES = 128
TT = 512
CT = 512
NEG = -3.0e38
VMEM_LIMIT = 60 * 1024 * 1024


def share_kernel(n, x_ref, out_ref, send_sem, recv_sem):
    me = lax.axis_index("tp")
    barrier = pltpu.get_barrier_semaphore()

    def greet(k, carry):
        pl.semaphore_signal(barrier, inc=1, device_id={"tp": lax.rem(me + k, n)}, device_id_type=MESH)
        return carry

    lax.fori_loop(1, n, greet, 0)
    pl.semaphore_wait(barrier, n - 1)

    def copy_to(k):
        peer = lax.rem(me + k, n)
        return pltpu.make_async_remote_copy(
            src_ref=x_ref,
            dst_ref=out_ref.at[me],
            send_sem=send_sem.at[peer],
            recv_sem=recv_sem.at[me],
            device_id={"tp": peer},
            device_id_type=MESH,
        )

    def start(k, carry):
        copy_to(k).start()
        return carry

    lax.fori_loop(1, n, start, 0)
    out_ref[me] = x_ref[...]

    def finish(k, carry):
        peer = lax.rem(me + k, n)
        copy_to(k).wait_send()
        pltpu.make_async_remote_copy(
            src_ref=x_ref,
            dst_ref=out_ref.at[peer],
            send_sem=send_sem.at[peer],
            recv_sem=recv_sem.at[peer],
            device_id={"tp": peer},
            device_id_type=MESH,
        ).wait_recv()
        return carry

    lax.fori_loop(1, n, finish, 0)


def share(x, n, ident):
    return pl.pallas_call(
        functools.partial(share_kernel, n),
        name=f"share{ident}",
        out_shape=jax.ShapeDtypeStruct((n, *x.shape), x.dtype),
        in_specs=[pl.BlockSpec(memory_space=pltpu.VMEM)],
        out_specs=pl.BlockSpec(memory_space=pltpu.VMEM),
        scratch_shapes=[pltpu.SemaphoreType.DMA((n,)), pltpu.SemaphoreType.DMA((n,))],
        compiler_params=pltpu.CompilerParams(collective_id=ident, has_side_effects=True),
    )(x)


def load_head(w_hbm, w_tail, w_scr, sem, start):
    width = w_scr.shape[1] - LANES
    a = pltpu.make_async_copy(w_hbm.at[:, pl.ds(0, width)], w_scr.at[:, pl.ds(0, width)], sem.at[0])
    b = pltpu.make_async_copy(w_tail, w_scr.at[:, pl.ds(width, LANES)], sem.at[1])
    for c in (a, b):
        if start:
            c.start()
        else:
            c.wait()


def fwd_kernel(vocab, x_ref, w_hbm, w_tail, z_ref, xt_ref, m_ref, s_ref, w_scr, zb0, zb1, sem):
    padded = w_scr.shape[1]
    tiles = padded // CT
    depth = x_ref.shape[1] // tiles

    @pl.when(pl.program_id(0) == 0)
    def _():
        load_head(w_hbm, w_tail, w_scr, sem, True)
        load_head(w_hbm, w_tail, w_scr, sem, False)

    m_ref[...] = jnp.full(m_ref.shape, NEG, jnp.float32)
    s_ref[...] = jnp.zeros(s_ref.shape, jnp.float32)
    lane = lax.broadcasted_iota(jnp.int32, (32, LANES), 1)

    def product(j, zb):
        zb[...] = jnp.dot(
            x_ref[...], w_scr[:, pl.ds(pl.multiple_of(j * CT, CT), CT)], preferred_element_type=jnp.float32
        )
        at = pl.ds(pl.multiple_of(j * depth, depth), depth)
        xt_ref[at, :] = x_ref[:, at].T

    def absorb(j, zb):
        last = CT // LANES - 1
        room = vocab - j * CT - last * LANES
        for r in range(0, TT, 32):
            rows = pl.ds(r, 32)
            zs = [zb[rows, pl.ds(k * LANES, LANES)] for k in range(CT // LANES)]
            for k in range(CT // LANES):
                z_ref[rows, pl.ds(pl.multiple_of(j * CT + k * LANES, LANES), LANES)] = zs[k]
            zs[last] = jnp.where(lane < room, zs[last], NEG)
            m_old = m_ref[rows, :]
            m_new = m_old
            for z in zs:
                m_new = jnp.maximum(m_new, z)
            total = s_ref[rows, :] * jnp.exp(m_old - m_new)
            for z in zs:
                total = total + jnp.exp(z - m_new)
            m_ref[rows, :] = m_new
            s_ref[rows, :] = total

    product(0, zb0)

    def pair(p, carry):
        product(2 * p + 1, zb1)
        absorb(2 * p, zb0)
        product(2 * p + 2, zb0)
        absorb(2 * p + 1, zb1)
        return carry

    lax.fori_loop(0, tiles // 2 - 1, pair, 0)
    product(tiles - 1, zb1)
    absorb(tiles - 2, zb0)
    absorb(tiles - 1, zb1)


def forward(x, w, w_tail):
    tokens, hidden = x.shape
    padded = w.shape[1] // LANES * LANES + LANES
    any_spec = pl.BlockSpec(memory_space=pl.ANY)
    return pl.pallas_call(
        functools.partial(fwd_kernel, w.shape[1]),
        name="forward",
        grid=(tokens // TT,),
        out_shape=(
            jax.ShapeDtypeStruct((tokens, padded), jnp.float32),
            jax.ShapeDtypeStruct((hidden, tokens), jnp.bfloat16),
            jax.ShapeDtypeStruct((tokens, LANES), jnp.float32),
            jax.ShapeDtypeStruct((tokens, LANES), jnp.float32),
        ),
        in_specs=[pl.BlockSpec((TT, hidden), lambda i: (i, 0)), any_spec, any_spec],
        out_specs=(
            pl.BlockSpec((TT, padded), lambda i: (i, 0)),
            pl.BlockSpec((hidden, TT), lambda i: (0, i)),
            pl.BlockSpec((TT, LANES), lambda i: (i, 0)),
            pl.BlockSpec((TT, LANES), lambda i: (i, 0)),
        ),
        scratch_shapes=[
            pltpu.VMEM((hidden, padded), jnp.bfloat16),
            pltpu.VMEM((TT, CT), jnp.float32),
            pltpu.VMEM((TT, CT), jnp.float32),
            pltpu.SemaphoreType.DMA((2,)),
        ],
        compiler_params=pltpu.CompilerParams(vmem_limit_bytes=VMEM_LIMIT),
        cost_estimate=pl.CostEstimate(flops=2 * tokens * hidden * padded, bytes_accessed=6 * tokens * padded, transcendentals=0),
    )(x, w, w_tail)


def grad_kernel(inv, z_ref, lse_ref, lab_ref, w_hbm, w_tail, g_ref, dx_ref, t_ref, w_scr, g0, g1, sem):
    padded = w_scr.shape[1]
    hidden = w_scr.shape[0]
    step = pl.program_id(0)
    steps = pl.num_programs(0)
    pieces = padded // CT
    width = hidden // pieces
    lane = lax.broadcasted_iota(jnp.int32, (32, LANES), 1)

    def probs(j, g):
        for r in range(0, TT, 32):
            rows = pl.ds(r, 32)
            lse = lse_ref[rows, :]
            rel = lab_ref[rows, :] - j * CT
            t = t_ref[...]
            for k in range(CT // LANES):
                at = pl.ds(pl.multiple_of(j * CT + k * LANES, LANES), LANES)
                z = z_ref[rows, at]
                p = jnp.exp(z - lse)
                hit = rel == lane + k * LANES
                t = t + jnp.where(hit, z, 0.0)
                gv = jnp.where(hit, p - inv, p).astype(jnp.bfloat16)
                g[rows, at] = gv
                g_ref[rows, at] = gv
            t_ref[...] = t

    @pl.when(step == 0)
    def _():
        load_head(w_hbm, w_tail, w_scr, sem, True)
        t_ref[...] = jnp.zeros(t_ref.shape, jnp.float32)

        def piece(j, carry):
            probs(j, g0)
            return carry

        lax.fori_loop(0, pieces, piece, 0)
        load_head(w_hbm, w_tail, w_scr, sem, False)

    def back(j, g):
        at = pl.ds(pl.multiple_of(j * width, width), width)
        dx_ref[:, at] = lax.dot_general(
            g[...], w_scr[at, :], (((1,), (1,)), ((), ())), preferred_element_type=jnp.float32
        )

    for parity, (now, later) in enumerate(((g1, g0), (g0, g1))):

        @pl.when((step > 0) & (step < steps - 1) & (lax.rem(step, 2) == parity))
        def _(now=now, later=later):
            def piece(j, carry):
                back(j, now)
                probs(j, later)
                return carry

            lax.fori_loop(0, pieces, piece, 0)

    @pl.when(step == steps - 1)
    def _():
        def piece(j, carry):
            back(j, g1)
            return carry

        lax.fori_loop(0, pieces, piece, 0)


def grad_rows(z, lse, lab, w, w_tail, inv):
    tokens, padded = z.shape
    hidden = w.shape[0]
    steps = tokens // TT
    any_spec = pl.BlockSpec(memory_space=pl.ANY)
    ahead = lambda i: (jnp.minimum(i, steps - 1), 0)
    return pl.pallas_call(
        functools.partial(grad_kernel, inv),
        name="grad_rows",
        grid=(steps + 1,),
        out_shape=(
            jax.ShapeDtypeStruct((tokens, padded), jnp.bfloat16),
            jax.ShapeDtypeStruct((tokens, hidden), jnp.float32),
            jax.ShapeDtypeStruct((32, LANES), jnp.float32),
        ),
        in_specs=[
            pl.BlockSpec((TT, padded), ahead),
            pl.BlockSpec((TT, LANES), ahead),
            pl.BlockSpec((TT, LANES), ahead),
            any_spec,
            any_spec,
        ],
        out_specs=(
            pl.BlockSpec((TT, padded), ahead),
            pl.BlockSpec((TT, hidden), lambda i: (jnp.maximum(i - 1, 0), 0)),
            pl.BlockSpec((32, LANES), lambda i: (0, 0)),
        ),
        scratch_shapes=[
            pltpu.VMEM((hidden, padded), jnp.bfloat16),
            pltpu.VMEM((TT, padded), jnp.bfloat16),
            pltpu.VMEM((TT, padded), jnp.bfloat16),
            pltpu.SemaphoreType.DMA((2,)),
        ],
        compiler_params=pltpu.CompilerParams(vmem_limit_bytes=VMEM_LIMIT),
        cost_estimate=pl.CostEstimate(flops=2 * tokens * hidden * padded, bytes_accessed=6 * tokens * padded, transcendentals=0),
    )(z, lse, lab, w, w_tail)


def head_kernel(xt_ref, g_ref, out_ref):
    def piece(j, carry):
        rows = pl.ds(pl.multiple_of(j * TT, TT), TT)
        out_ref[rows, :] = jnp.dot(xt_ref[rows, :], g_ref[...], preferred_element_type=jnp.float32).astype(jnp.bfloat16)
        return carry

    lax.fori_loop(0, xt_ref.shape[0] // TT, piece, 0)


def grad_head(xt, g, vocab):
    hidden, tokens = xt.shape
    padded = g.shape[1]
    width = 256
    return pl.pallas_call(
        head_kernel,
        name="grad_head",
        grid=(padded // width,),
        out_shape=jax.ShapeDtypeStruct((hidden, vocab), jnp.bfloat16),
        in_specs=[
            pl.BlockSpec((hidden, tokens), lambda i: (0, 0), pipeline_mode=pl.Buffered(1)),
            pl.BlockSpec((tokens, width), lambda i: (0, i)),
        ],
        out_specs=pl.BlockSpec((hidden, width), lambda i: (0, i)),
        compiler_params=pltpu.CompilerParams(vmem_limit_bytes=VMEM_LIMIT),
        cost_estimate=pl.CostEstimate(flops=2 * tokens * hidden * padded, bytes_accessed=4 * tokens * padded, transcendentals=0),
    )(xt, g)


def solution(mesh):
    n = mesh.shape["tp"]

    def local_step(hid_loc, w_loc, lab_loc):
        rows, hidden = hid_loc.shape
        vocab = w_loc.shape[1]
        tokens = rows * n
        inv = 1.0 / tokens
        even = vocab // LANES * LANES
        w_tail = jnp.pad(w_loc[:, even:], ((0, 0), (0, even + LANES - vocab)))
        lab_all = share(jnp.broadcast_to(lab_loc.reshape(1, rows), (8, rows)), n, 0)[:, 0, :]
        hid_all = lax.all_gather(hid_loc, "tp", axis=0, tiled=True)
        z, xt, m_lane, s_lane = forward(hid_all, w_loc, w_tail)
        m_loc = jnp.max(m_lane, axis=1)
        s_loc = jnp.sum(s_lane * jnp.exp(m_lane - m_loc[:, None]), axis=1)
        stats = share(jnp.concatenate([m_loc.reshape(-1, LANES), s_loc.reshape(-1, LANES)]), n, 1)
        m_all, s_all = stats[:, : tokens // LANES], stats[:, tokens // LANES :]
        m_glob = jnp.max(m_all, axis=0)
        s_glob = jnp.sum(s_all * jnp.exp(m_all - m_glob), axis=0)
        lse = m_glob + jnp.log(s_glob)
        lse_b = jnp.broadcast_to((lse + math.log(tokens)).reshape(tokens, 1), (tokens, LANES))
        lab_b = jnp.broadcast_to((lab_all.reshape(tokens, 1) - lax.axis_index("tp") * vocab), (tokens, LANES))
        g, dx, t = grad_rows(z, lse_b, lab_b, w_loc, w_tail, inv)
        d_head = grad_head(xt, g, vocab)
        d_hidden = lax.psum_scatter(dx, "tp", scatter_dimension=0, tiled=True)
        hit_sum = jnp.sum(share(jnp.sum(t.reshape(4, 8, LANES), axis=0), n, 2))
        mean_loss = ((jnp.sum(lse) - hit_sum) * inv).reshape(1)
        return mean_loss, d_hidden.astype(jnp.bfloat16), d_head

    return jax.shard_map(
        local_step,
        mesh=mesh,
        in_specs=(P(("dp", "tp"), None), P(None, "tp"), P(("dp", "tp"))),
        out_specs=(P("dp"), P(("dp", "tp"), None), P("dp", "tp")),
        check_vma=False,
    )
```

time: 550 us -> 493 us (0.90)
  Pallas kernels: 0 us -> 344 us
  matrix products: 237 us -> 0 us
  blocking collectives: 122 us -> 0 us
  local copies, waits for them, and re-layouts: 0.03 us -> 51.6 us
  waiting for transfers between devices: 117 us -> 66.1 us
  other arithmetic: 57.9 us -> 13.6 us
    pallas_call x0 -> x6, Pallas kernels: none -> 344 us  [the longest x1 115 us: grad_rows(): pl.pallas_call(functools.partial(grad_kernel, inv), name='grad_rows', gri...]
    dot_general x3 -> x0, matrix products: 237 us -> none  [the longest x1 80.6 us: local_step(): lax.dot_general(grad_out, w_loc, (((1,), (1,)), ((), ())), preferred_elem...]
    pmax x1 -> x0, blocking collectives: 44.9 us -> none  [local_step(): glob_max = lax.pmax(jnp.max(logits, axis=1), 'tp')]
    psum x1 -> x0, blocking collectives: 44.7 us -> none  [local_step(): stat_sums = lax.psum(local_stats, 'tp')]
    reduce_scatter x1, waiting for transfers between devices: 75.6 us -> 31.7 us  [local_step(): d_hidden = lax.psum_scatter(dx, 'tp', scatter_dimension=0, tiled=True)]
    unnamed x2 -> x6, local copies, waits for them, and re-layouts: 0.01 us -> 43.5 us
    convert_element_type x2 -> x1, other arithmetic: 35.3 us -> 2.08 us  [local_step(): return (mean_loss, d_hidden.astype(jnp.bfloat16), d_head)]
    all_gather x1 -> x0, blocking collectives: 32.2 us -> none  [local_step(): lab_all = lax.all_gather(lab_loc, 'tp', axis=0, tiled=True)]
  transfers between devices with their start and end apart: 2 -> 2, of which waited for: 2 -> 2; matrix products, arithmetic and copies ran while one was open for 14% -> 10% of each run, Pallas kernels for 0% -> 23%
where the time goes in v1:
time: 493 us; the launch traced here: 492 us
  Pallas kernels  344 us (70%)
  waiting for transfers between devices  66.1 us (13%)
  local copies, waits for them, and re-layouts  51.6 us (10%)
  between operations  16.6 us (3%)
  other arithmetic  13.6 us (3%)
    pallas_call x1, Pallas kernels, grad_rows(): pl.pallas_call(functools.partial(grad_kernel, inv), name='grad_rows', gri...  115 us
    pallas_call x1, Pallas kernels, forward(): pl.pallas_call(functools.partial(fwd_kernel, w.shape[1]), name='forward',...  92.2 us
    pallas_call x1, Pallas kernels, grad_head(): pl.pallas_call(head_kernel, name='grad_head', grid=(padded // width,), ou...  87.9 us
    pallas_call x3, Pallas kernels, share(): pl.pallas_call(functools.partial(share_kernel, n), name=f'share{ident}',...  48.2 us
    unnamed x6, local copies, waits for them, and re-layouts  43.5 us
    all_gather x1, waiting for transfers between devices, local_step(): hid_all = lax.all_gather(hid_loc, 'tp', axis=0, tiled=True)  33.6 us
    reduce_scatter x1, waiting for transfers between devices, local_step(): d_hidden = lax.psum_scatter(dx, 'tp', scatter_dimension=0, tiled=True)  31.7 us
  transfers between devices with their start and end apart: 2, of which 2 were waited for; matrix products, arithmetic and copies ran while one was open for 10% of the time, Pallas kernels for 23%

profile of v1, /device:TPU:97, one launch (start us, length us, event | category | flops | bytes accessed | tf_op | source)
XLA Modules:
  0.0 491.6 jit_solution(3733373336353770115)
XLA Ops:
  7.2 0.1 all-gather.2.cloned.1.call-start
  7.2 0.7 all-gather.2.cloned.1.call-update
  8.0 0.1 reduce-scatter.2.cloned.1.call-start
  8.0 1.2 broadcast_in_dim.7.x_ref
  9.3 14.7 %share0.1 = s32[32,8,128]{2,1,0:T(8,128)} custom-call(s32[8,128]{1,0:T(8,128)} %broadcast_in_dim.7.x_ref), custom_call_target="tpu_custom_call" | custom-call | tf_op jit(solution)/shard_map/share0/pallas_call | solution.py:65
  24.0 21.1 %copy.7.w_hbm = bf16[2048,4008]{1,0:T(8,128)(2,1)} copy(bf16[2048,4008]{0,1:T(8,128)(2,1)} %param.4) | data formatting | bytes 32833536 | tf_op args[1]
  45.2 1.1 slice.16
  46.3 0.9 pad.4.w_tail
  47.2 0.9 slice_subtract_fusion
  48.1 33.6 %all-gather.2.cloned.1.call-done.x_ref = bf16[4096,2048]{1,0:T(8,128)(2,1)} async-done(((bf16[128,2048]{1,0:T(8,128)(2,1)}), bf16[4096,2048]{1,0:T(8,128)(2,1)}) %all-gather.2.cloned.1.call-update) | async-done | bytes 16777232 | tf_op jit(solution)/shard_map/all_gather | solution.py:315
  81.7 92.2 %forward.1 = (f32[4096,4096]{1,0:T(8,128)}, bf16[2048,4096]{1,0:T(8,128)(2,1)}, f32[4096,128]{1,0:T(8,128)}, f32[4096,128]{1,0:T(8,128)}) custom-call(bf16[4096,2048]{1,0:T(8,128)(2,1)} %all-gather.2.cloned.1.call-done.x_ref, bf16[2048,4008]{1,0:T(8,128)(2,1)} %copy.7.w_hbm, bf16[2048,128]{1,0:T(8,128)(2,1)} %pad.4.w_tail), custom_call_target="tpu_custom_call" | custom-call | flops 68719476736 | bytes 100663296 | tf_op jit(solution)/shard_map/forward/pallas_call | solution.py:146
  173.8 0.0 copy-start
  173.9 2.4 reduce_max.18
  176.2 0.0 copy-done
  176.2 2.5 multiply_reduce_fusion
  178.7 0.6 pad_maximum_fusion.x_ref
  179.3 22.4 %share1.1 = f32[32,64,128]{2,1,0:T(8,128)} custom-call(f32[64,128]{1,0:T(8,128)} %pad_maximum_fusion.x_ref), custom_call_target="tpu_custom_call" | custom-call | tf_op jit(solution)/shard_map/share1/pallas_call | solution.py:65
  201.8 1.1 slice_reduce_fusion
  202.9 1.3 multiply_reduce_fusion.1
  204.2 0.6 add_bitcast_fusion
  204.8 2.9 broadcast_in_dim.8.lab_ref
  207.7 1.9 broadcast_in_dim.6.lse_ref
  209.7 115.3 %grad_rows.1 = (bf16[4096,4096]{1,0:T(8,128)(2,1)}, f32[4096,2048]{1,0:T(8,128)}, f32[32,128]{1,0:T(8,128)}) custom-call(f32[4096,4096]{1,0:T(8,128)} %get-tuple-element.12.z_ref, f32[4096,128]{1,0:T(8,128)} %broadcast_in_dim.6.lse_ref, s32[4096,128]{1,0:T(8,128)} %broadcast_in_dim.8.lab_ref, bf16[2048,4008]{1,0:T(8,128)(2,1)} %copy.7.w_hbm, ...), custom_call_target="tpu_custom_call" | custom-call | flops 68719476736 | bytes 100663296 | tf_op jit(solution)/shard_map/grad_rows/pallas_call | solution.py:244
  324.9 0.1 reduce-scatter.2.cloned.1.call-update
  325.0 87.9 %grad_head.1 = bf16[2048,4008]{1,0:T(8,128)(2,1)} custom-call(bf16[2048,4096]{1,0:T(8,128)(2,1)} %get-tuple-element.15.xt_ref, bf16[4096,4096]{1,0:T(8,128)(2,1)} %get-tuple-element.16.g_ref), custom_call_target="tpu_custom_call" | custom-call | flops 68719476736 | bytes 67108864 | tf_op jit(solution)/shard_map/grad_head/pallas_call | solution.py:289
  412.9 0.0 copy-start.1
  412.9 22.4 %copy.9 = bf16[2048,4008]{0,1:T(8,128)(2,1)} copy(bf16[2048,4008]{1,0:T(8,128)(2,1)} %grad_head.1) | data formatting | bytes 32833536
  435.3 0.0 copy-done.1
  435.3 0.6 bitcast_reduce_fusion.x_ref
  435.9 11.0 %share2.1 = f32[32,8,128]{2,1,0:T(8,128)} custom-call(f32[8,128]{1,0:T(8,128)} %bitcast_reduce_fusion.x_ref), custom_call_target="tpu_custom_call" | custom-call | tf_op jit(solution)/shard_map/share2/pallas_call | solution.py:65
  447.0 1.5 reduce_sum.49
  449.8 31.7 %reduce-scatter.2.cloned.1.call-done = f32[128,2048]{1,0:T(8,128)} async-done(((f32[4096,2048]{1,0:T(8,128)}), f32[128,2048]{1,0:T(8,128)}) %reduce-scatter.2.cloned.1.call-update) | async-done | bytes 1048592 | tf_op jit(solution)/shard_map/reduce_scatter | solution.py:328
  481.5 2.1 convert_element_type.5
Async XLA Ops:
  7.2 74.5 %all-gather.2.cloned.1.call-start = ((), (), s32[]{:S(2)}) async-start(), calls=%async_computation.1 | async-start | bytes 17301504 | tf_op jit(solution)/shard_map/all_gather | solution.py:315
  8.0 473.6 %reduce-scatter.2.cloned.1.call-start = ((), (), s32[]{:S(2)}) async-start(), calls=%async_computation.2 | async-start | bytes 34603008 | tf_op jit(solution)/shard_map/reduce_scatter | solution.py:328
  173.8 2.4 copy-start
  412.9 22.4 %copy-start.1 = (f32[32,128]{1,0:T(8,128)S(1)}, f32[32,128]{1,0:T(8,128)}, u32[]{:S(2)}) copy-start(f32[32,128]{1,0:T(8,128)} %get-tuple-element.13) | copy-start | bytes 49156
Sparse Core Ops, SparseCore 0:
  10.1 71.5 all-gather.1
  325.1 156.3 reduce-scatter.1

commit v2 on v1

v2 whole, which is shorter than its diff:
```python
import functools
import math

import jax
import jax.numpy as jnp
from jax import lax
from jax.experimental import pallas as pl
from jax.experimental.pallas import tpu as pltpu
from jax.sharding import PartitionSpec as P

MESH = pl.DeviceIdType.MESH
LANES = 128
TT = 512
CT = 512
NEG = -3.0e38
VMEM_LIMIT = 60 * 1024 * 1024


def share_kernel(n, x_ref, out_ref, send_sem, recv_sem):
    me = lax.axis_index("tp")
    barrier = pltpu.get_barrier_semaphore()

    def greet(k, carry):
        pl.semaphore_signal(barrier, inc=1, device_id={"tp": lax.rem(me + k, n)}, device_id_type=MESH)
        return carry

    lax.fori_loop(1, n, greet, 0)
    pl.semaphore_wait(barrier, n - 1)

    def copy_to(k):
        peer = lax.rem(me + k, n)
        return pltpu.make_async_remote_copy(
            src_ref=x_ref,
            dst_ref=out_ref.at[me],
            send_sem=send_sem.at[peer],
            recv_sem=recv_sem.at[me],
            device_id={"tp": peer},
            device_id_type=MESH,
        )

    def start(k, carry):
        copy_to(k).start()
        return carry

    lax.fori_loop(1, n, start, 0)
    out_ref[me] = x_ref[...]

    def finish(k, carry):
        peer = lax.rem(me + k, n)
        copy_to(k).wait_send()
        pltpu.make_async_remote_copy(
            src_ref=x_ref,
            dst_ref=out_ref.at[peer],
            send_sem=send_sem.at[peer],
            recv_sem=recv_sem.at[peer],
            device_id={"tp": peer},
            device_id_type=MESH,
        ).wait_recv()
        return carry

    lax.fori_loop(1, n, finish, 0)


def share(x, n, ident):
    return pl.pallas_call(
        functools.partial(share_kernel, n),
        name=f"share{ident}",
        out_shape=jax.ShapeDtypeStruct((n, *x.shape), x.dtype),
        in_specs=[pl.BlockSpec(memory_space=pltpu.VMEM)],
        out_specs=pl.BlockSpec(memory_space=pltpu.VMEM),
        scratch_shapes=[pltpu.SemaphoreType.DMA((n,)), pltpu.SemaphoreType.DMA((n,))],
        compiler_params=pltpu.CompilerParams(collective_id=ident, has_side_effects=True),
    )(x)


def combine_kernel(n, stat_ref, mine_ref, out_ref, got, row, send_a, recv_a, send_b, recv_b):
    me = lax.axis_index("tp")
    barrier = pltpu.get_barrier_semaphore()

    def each(body):
        def step(k, carry):
            body(lax.rem(me + k, n))
            return carry

        lax.fori_loop(1, n, step, 0)

    each(lambda peer: pl.semaphore_signal(barrier, inc=1, device_id={"tp": peer}, device_id_type=MESH))
    pl.semaphore_wait(barrier, n - 1)

    def copy(src, dst, send, recv, peer):
        return pltpu.make_async_remote_copy(
            src_ref=src, dst_ref=dst, send_sem=send, recv_sem=recv, device_id={"tp": peer}, device_id_type=MESH
        )

    def first(peer, slot):
        return copy(stat_ref.at[peer], got.at[slot], send_a.at[peer], recv_a.at[slot], peer)

    def second(peer, slot):
        return copy(row, out_ref.at[slot], send_b.at[peer], recv_b.at[slot], peer)

    each(lambda peer: first(peer, me).start())
    got[me] = stat_ref[me]
    each(lambda peer: first(peer, peer).wait_recv())
    m_all = got[:, 0, :]
    top = jnp.max(m_all, axis=0, keepdims=True)
    total = jnp.sum(got[:, 1, :] * jnp.exp(m_all - top), axis=0, keepdims=True)
    lse = top + jnp.log(total)
    first_row = lax.broadcasted_iota(jnp.int32, row.shape, 0) == 0
    mixed = jnp.where(first_row, jnp.broadcast_to(lse, row.shape), mine_ref[...])
    row[...] = mixed
    out_ref[me] = mixed
    each(lambda peer: second(peer, me).start())
    each(lambda peer: first(peer, me).wait_send())
    each(lambda peer: second(peer, peer).wait_recv())
    each(lambda peer: second(peer, me).wait_send())


def combine(stat, mine, n, ident):
    vmem = pl.BlockSpec(memory_space=pltpu.VMEM)
    return pl.pallas_call(
        functools.partial(combine_kernel, n),
        name="combine",
        out_shape=jax.ShapeDtypeStruct(stat.shape, stat.dtype),
        in_specs=[vmem, vmem],
        out_specs=vmem,
        scratch_shapes=[pltpu.VMEM(stat.shape, stat.dtype), pltpu.VMEM(mine.shape, mine.dtype)]
        + [pltpu.SemaphoreType.DMA((n,))] * 4,
        compiler_params=pltpu.CompilerParams(collective_id=ident, has_side_effects=True),
    )(stat, mine)


ORDER = [(0, 0), (1, 0), (3, 0), (0, 1), (0, 3), (2, 0), (0, 2), (1, 1)]
ORDER += [(1, 3), (3, 1), (3, 3), (2, 1), (2, 3), (1, 2), (3, 2), (2, 2)]
PLACE = {at: k for k, at in enumerate(ORDER)}
WT = 256


def fwd_kernel(n, x_ref, wt_hbm, z_ref, xt_ref, m_ref, s_ref, w_scr, x_all, stage, zb0, zb1, wsem, send, recv, pair_send, pair_recv):
    side = math.isqrt(n // 2)
    vocab, hidden = wt_hbm.shape
    padded = w_scr.shape[1]
    rows = x_ref.shape[0]
    half = rows // 2
    tiles = padded // CT
    depth = hidden // tiles
    step = pl.program_id(0)
    me = lax.axis_index("tp")
    core = lax.rem(me, 2)
    chip = me // 2
    x, y = lax.rem(chip, side), chip // side
    p, q = x + core * (y - x), y + core * (x - y)

    def device(dp, dq):
        pp, qq = lax.rem(p + dp, side), lax.rem(q + dq, side)
        return ((qq + core * (pp - qq)) * side + pp + core * (qq - pp)) * 2 + core

    def place(dp, dq):
        dp, dq = dp % side, dq % side
        a, b = PLACE[dp, dq], PLACE[dq, dp]
        return a + core * (b - a)

    def view(dp, dq, lo, count):
        return x_all.at[pl.ds(pl.multiple_of((place(dp, dq) * 2 + core) * rows + lo, half), count), :]

    def slot(dp, dq, lo):
        return ((dp % side) * side + dq % side) * 2 + (1 if lo else 0)

    sent = []

    def ici(number, dp, dq, axis, sign, lo, count):
        to = (sign, 0) if axis == "p" else (0, sign)
        rp, rq = dp - to[0], dq - to[1]
        src = x_ref if (dp, dq) == (0, 0) else view(dp, dq, lo, count)
        return pltpu.make_async_remote_copy(
            src_ref=src,
            dst_ref=view(rp, rq, lo, count),
            send_sem=send.at[number],
            recv_sem=recv.at[slot(rp, rq, lo)],
            device_id={"tp": device(to[0] % side, to[1] % side)},
            device_id_type=MESH,
        )

    def put(*args):
        ici(len(sent), *args).start()
        sent.append(args)

    def got(dp, dq, lo, count):
        v = view(dp, dq, lo, count)
        pltpu.make_async_remote_copy(
            src_ref=v, dst_ref=v, send_sem=send.at[0], recv_sem=recv.at[slot(dp, dq, lo)],
            device_id={"tp": me}, device_id_type=MESH,
        ).wait_recv()

    pair_sent = []

    def pair_copy(dp, dq):
        v = view(dp, dq, 0, rows)
        at = place(dp, dq)
        return pltpu.make_async_remote_copy(
            src_ref=x_ref if (dp, dq) == (0, 0) else v, dst_ref=v, send_sem=pair_send.at[at], recv_sem=pair_recv.at[at],
            device_id={"tp": me + 1 - 2 * core}, device_id_type=MESH,
        )

    def pair(dp, dq):
        pair_copy(dp, dq).start()
        pair_sent.append((dp, dq))

    def pair_got(at):
        v = x_all.at[pl.ds(pl.multiple_of((at * 2 + 1 - core) * rows, half), rows), :]
        pltpu.make_async_remote_copy(
            src_ref=v, dst_ref=v, send_sem=pair_send.at[at], recv_sem=pair_recv.at[at],
            device_id={"tp": me + 1 - 2 * core}, device_id_type=MESH,
        ).wait_recv()

    def near_q(dp):
        got(dp, -1, 0, rows)
        put(dp, -1, "q", 1, 0, half)
        got(dp, 1, 0, rows)
        put(dp, 1, "q", -1, half, half)
        pair(dp, -1)
        pair(dp, 1)

    def far_q(dp):
        got(dp, 2, 0, half)
        got(dp, 2, half, half)
        pair(dp, 2)

    def both_q(dp):
        put(dp, 0, "q", 1, 0, rows)
        put(dp, 0, "q", -1, 0, rows)

    def head_copy(t, count):
        return pltpu.make_async_copy(
            wt_hbm.at[pl.ds(pl.multiple_of(t * WT, WT), count), :],
            stage.at[lax.rem(t, 2), pl.ds(0, count), :],
            wsem.at[lax.rem(t, 2)],
        )

    whole = vocab // WT
    rest = vocab - whole * WT

    def turn(lo, hi):
        def body(t, carry):
            head_copy(t, WT).wait()
            w_scr[:, pl.ds(pl.multiple_of(t * WT, WT), WT)] = stage[lax.rem(t, 2)].T

            @pl.when(t + 2 < whole)
            def _():
                head_copy(t + 2, WT).start()

            @pl.when(t + 2 == whole)
            def _():
                head_copy(whole, rest).start()

            return carry

        lax.fori_loop(lo, hi, body, 0)

    def services(k):
        if k == 0:
            barrier = pltpu.get_barrier_semaphore()
            for peer in (device(1, 0), device(side - 1, 0), device(0, 1), device(0, side - 1), me + 1 - 2 * core):
                pl.semaphore_signal(barrier, inc=1, device_id={"tp": peer}, device_id_type=MESH)
            head_copy(0, WT).start()
            head_copy(1, WT).start()
            pl.semaphore_wait(barrier, 5)
            put(0, 0, "p", 1, 0, rows)
            put(0, 0, "p", -1, 0, rows)
            pair(0, 0)
            both_q(0)
            x_all[pl.ds(pl.multiple_of(core * rows, rows), rows), :] = x_ref[...]
            turn(0, whole // 3)
            got(-1, 0, 0, rows)
            put(-1, 0, "p", 1, 0, half)
            got(1, 0, 0, rows)
            put(1, 0, "p", -1, half, half)
            pair(-1, 0)
            pair(1, 0)
            both_q(1)
            both_q(-1)
            turn(whole // 3, 2 * whole // 3)
            got(2, 0, 0, half)
            got(2, 0, half, half)
            pair(2, 0)
            both_q(2)
            near_q(0)
            turn(2 * whole // 3, whole)
            stage[whole % 2, pl.ds(rest, WT - rest), :] = jnp.zeros((WT - rest, hidden), jnp.bfloat16)
            head_copy(whole, rest).wait()
            w_scr[:, pl.ds(whole * WT, WT)] = stage[whole % 2].T
        if k == 1:
            near_q(1)
            far_q(0)
        if k == 2:
            near_q(-1)
            far_q(1)
        if k == 3:
            near_q(2)
            far_q(-1)
        if k == 4:
            far_q(2)
        pair_got(2 * k)
        pair_got(2 * k + 1)

    @pl.when(step == 0)
    def _():
        services(0)

    m_ref[...] = jnp.full(m_ref.shape, NEG, jnp.float32)
    s_ref[...] = jnp.zeros(s_ref.shape, jnp.float32)
    lane = lax.broadcasted_iota(jnp.int32, (32, LANES), 1)
    here = pl.ds(pl.multiple_of(step * TT, TT), TT)

    def product(j, zb):
        zb[...] = jnp.dot(
            x_all[here, :], w_scr[:, pl.ds(pl.multiple_of(j * CT, CT), CT)], preferred_element_type=jnp.float32
        )
        at = pl.ds(pl.multiple_of(j * depth, depth), depth)
        xt_ref[at, :] = x_all[here, at].T

    def absorb(j, zb):
        last = CT // LANES - 1
        room = vocab - j * CT - last * LANES
        for r in range(0, TT, 32):
            part = pl.ds(r, 32)
            zs = [zb[part, pl.ds(k * LANES, LANES)] for k in range(CT // LANES)]
            for k in range(CT // LANES):
                z_ref[part, pl.ds(pl.multiple_of(j * CT + k * LANES, LANES), LANES)] = zs[k]
            zs[last] = jnp.where(lane < room, zs[last], NEG)
            m_old = m_ref[part, :]
            m_new = m_old
            for z in zs:
                m_new = jnp.maximum(m_new, z)
            total = s_ref[part, :] * jnp.exp(m_old - m_new)
            for z in zs:
                total = total + jnp.exp(z - m_new)
            m_ref[part, :] = m_new
            s_ref[part, :] = total

    product(0, zb0)

    def two(k, carry):
        product(2 * k + 1, zb1)
        absorb(2 * k, zb0)
        product(2 * k + 2, zb0)
        absorb(2 * k + 1, zb1)
        return carry

    lax.fori_loop(0, tiles // 2 - 1, two, 0)
    for k in range(1, len(ORDER) // 2):

        @pl.when(step == k - 1)
        def _(k=k):
            services(k)

    product(tiles - 1, zb1)
    absorb(tiles - 2, zb0)
    absorb(tiles - 1, zb1)

    @pl.when(step == pl.num_programs(0) - 1)
    def _():
        for number, args in enumerate(sent):
            ici(number, *args).wait_send()
        for args in pair_sent:
            pair_copy(*args).wait_send()


def forward(x, wt, n, ident):
    rows, hidden = x.shape
    tokens = rows * n
    padded = wt.shape[0] // LANES * LANES + LANES
    copies = 2 + 2 + 2 * 4 + 2 * 4
    return pl.pallas_call(
        functools.partial(fwd_kernel, n),
        name="forward",
        grid=(tokens // TT,),
        out_shape=(
            jax.ShapeDtypeStruct((tokens, padded), jnp.float32),
            jax.ShapeDtypeStruct((hidden, tokens), jnp.bfloat16),
            jax.ShapeDtypeStruct((tokens, LANES), jnp.float32),
            jax.ShapeDtypeStruct((tokens, LANES), jnp.float32),
        ),
        in_specs=[
            pl.BlockSpec((rows, hidden), lambda i: (0, 0), pipeline_mode=pl.Buffered(1)),
            pl.BlockSpec(memory_space=pl.ANY),
        ],
        out_specs=(
            pl.BlockSpec((TT, padded), lambda i: (i, 0)),
            pl.BlockSpec((hidden, TT), lambda i: (0, i)),
            pl.BlockSpec((TT, LANES), lambda i: (i, 0)),
            pl.BlockSpec((TT, LANES), lambda i: (i, 0)),
        ),
        scratch_shapes=[
            pltpu.VMEM((hidden, padded), jnp.bfloat16),
            pltpu.VMEM((tokens, hidden), jnp.bfloat16),
            pltpu.VMEM((2, WT, hidden), jnp.bfloat16),
            pltpu.VMEM((TT, CT), jnp.float32),
            pltpu.VMEM((TT, CT), jnp.float32),
            pltpu.SemaphoreType.DMA((2,)),
            pltpu.SemaphoreType.DMA((copies,)),
            pltpu.SemaphoreType.DMA((n,)),
            pltpu.SemaphoreType.DMA((n // 2,)),
            pltpu.SemaphoreType.DMA((n // 2,)),
        ],
        compiler_params=pltpu.CompilerParams(
            vmem_limit_bytes=67_043_328, collective_id=ident, has_side_effects=True
        ),
        cost_estimate=pl.CostEstimate(flops=2 * tokens * hidden * padded, bytes_accessed=6 * tokens * padded, transcendentals=0),
    )(x, wt)


def grad_kernel(inv, chips_ref, z_ref, lse_ref, lab_ref, wt_hbm, g_ref, dx_hbm, t_ref, w_scr, g0, g1, dx0, dx1, sem, out_sem):
    padded, hidden = w_scr.shape
    vocab = wt_hbm.shape[0]
    step = pl.program_id(0)
    steps = pl.num_programs(0)
    pieces = padded // CT
    width = hidden // pieces
    lane = lax.broadcasted_iota(jnp.int32, (32, LANES), 1)

    def probs(j, g):
        for r in range(0, TT, 32):
            rows = pl.ds(r, 32)
            lse = lse_ref[rows, :]
            rel = lab_ref[rows, :] - j * CT
            t = t_ref[...]
            for k in range(CT // LANES):
                at = pl.ds(pl.multiple_of(j * CT + k * LANES, LANES), LANES)
                z = z_ref[rows, at]
                p = jnp.exp(z - lse)
                hit = rel == lane + k * LANES
                t = t + jnp.where(hit, z, 0.0)
                gv = jnp.where(hit, p - inv, p).astype(jnp.bfloat16)
                g[rows, at] = gv
                g_ref[rows, at] = gv
            t_ref[...] = t

    @pl.when(step == 0)
    def _():
        load = pltpu.make_async_copy(wt_hbm, w_scr.at[pl.ds(0, vocab), :], sem)
        load.start()
        w_scr[pl.ds(vocab, padded - vocab), :] = jnp.zeros((padded - vocab, hidden), jnp.bfloat16)
        t_ref[...] = jnp.zeros(t_ref.shape, jnp.float32)

        def piece(j, carry):
            probs(j, g0)
            return carry

        lax.fori_loop(0, pieces, piece, 0)
        load.wait()

    per_chip = TT // 2

    def leave(at, dx):
        return [
            pltpu.make_async_copy(
                dx.at[pl.ds(k * per_chip, per_chip), :],
                dx_hbm.at[pl.ds(pl.multiple_of(chips_ref[at * 2 + k] * per_chip, per_chip), per_chip), :],
                out_sem.at[lax.rem(at, 2), k],
            )
            for k in range(2)
        ]

    def back(j, g, dx):
        at = pl.ds(pl.multiple_of(j * width, width), width)
        dx[:, at] = jnp.dot(g[...], w_scr[:, at], preferred_element_type=jnp.float32)

    for parity, (now, later, dx) in enumerate(((g1, g0, dx1), (g0, g1, dx0))):

        @pl.when((step > 2) & (lax.rem(step, 2) == parity))
        def _(dx=dx):
            for c in leave(step - 3, dx):
                c.wait()

        @pl.when((step > 0) & (step < steps - 1) & (lax.rem(step, 2) == parity))
        def _(now=now, later=later, dx=dx):
            def piece(j, carry):
                back(j, now, dx)
                probs(j, later)
                return carry

            lax.fori_loop(0, pieces, piece, 0)

        if parity == 0:

            @pl.when(step == steps - 1)
            def _(now=now, dx=dx):
                def piece(j, carry):
                    back(j, now, dx)
                    return carry

                lax.fori_loop(0, pieces, piece, 0)

        @pl.when((step > 0) & (lax.rem(step, 2) == parity))
        def _(dx=dx):
            for c in leave(step - 1, dx):
                c.start()

    @pl.when(step == steps - 1)
    def _():
        for c in leave(step - 2, dx0) + leave(step - 1, dx1):
            c.wait()


def grad_rows(chips, z, lse, lab, wt, inv):
    tokens, padded = z.shape
    hidden = wt.shape[1]
    steps = tokens // TT
    ahead = lambda i: (jnp.minimum(i, steps - 1), 0)
    return pl.pallas_call(
        functools.partial(grad_kernel, inv),
        name="grad_rows",
        grid=(steps + 1,),
        out_shape=(
            jax.ShapeDtypeStruct((tokens, padded), jnp.bfloat16),
            jax.ShapeDtypeStruct((tokens, hidden), jnp.float32),
            jax.ShapeDtypeStruct((32, LANES), jnp.float32),
        ),
        in_specs=[
            pl.BlockSpec(memory_space=pltpu.SMEM),
            pl.BlockSpec((TT, padded), ahead),
            pl.BlockSpec((TT, LANES), ahead),
            pl.BlockSpec((TT, LANES), ahead),
            pl.BlockSpec(memory_space=pl.ANY),
        ],
        out_specs=(
            pl.BlockSpec((TT, padded), ahead),
            pl.BlockSpec(memory_space=pl.ANY),
            pl.BlockSpec((32, LANES), lambda i: (0, 0)),
        ),
        scratch_shapes=[
            pltpu.VMEM((padded, hidden), jnp.bfloat16),
            pltpu.VMEM((TT, padded), jnp.bfloat16),
            pltpu.VMEM((TT, padded), jnp.bfloat16),
            pltpu.VMEM((TT, hidden), jnp.float32),
            pltpu.VMEM((TT, hidden), jnp.float32),
            pltpu.SemaphoreType.DMA,
            pltpu.SemaphoreType.DMA((2, 2)),
        ],
        compiler_params=pltpu.CompilerParams(vmem_limit_bytes=VMEM_LIMIT),
        cost_estimate=pl.CostEstimate(flops=2 * tokens * hidden * padded, bytes_accessed=6 * tokens * padded, transcendentals=0),
    )(chips, z, lse, lab, wt)


def head_kernel(parts, *refs):
    xts, gs, out_ref = refs[:parts], refs[parts : 2 * parts], refs[2 * parts]

    def piece(j, carry):
        rows = pl.ds(pl.multiple_of(j * TT, TT), TT)
        total = None
        for xt, g in zip(xts, gs):
            term = jnp.dot(xt[rows, :], g[...], preferred_element_type=jnp.float32)
            total = term if total is None else total + term
        out_ref[:, rows] = total.astype(jnp.bfloat16).T
        return carry

    lax.fori_loop(0, out_ref.shape[1] // TT, piece, 0)


def grad_head(xts, gs, vocab):
    hidden = xts[0].shape[0]
    tokens = sum(x.shape[1] for x in xts)
    padded = gs[0].shape[1]
    width = 256
    return pl.pallas_call(
        functools.partial(head_kernel, len(xts)),
        name="grad_head",
        grid=(padded // width,),
        out_shape=jax.ShapeDtypeStruct((vocab, hidden), jnp.bfloat16),
        in_specs=[pl.BlockSpec(x.shape, lambda i: (0, 0), pipeline_mode=pl.Buffered(1)) for x in xts]
        + [pl.BlockSpec((g.shape[0], width), lambda i: (0, i)) for g in gs],
        out_specs=pl.BlockSpec((width, hidden), lambda i: (i, 0)),
        compiler_params=pltpu.CompilerParams(vmem_limit_bytes=VMEM_LIMIT),
        cost_estimate=pl.CostEstimate(flops=2 * tokens * hidden * padded, bytes_accessed=4 * tokens * padded, transcendentals=0),
    )(*xts, *gs)


def solution(mesh):
    n = mesh.shape["tp"]

    def local_step(hid_loc, w_loc, lab_loc):
        rows, hidden = hid_loc.shape
        vocab = w_loc.shape[1]
        tokens = rows * n
        inv = 1.0 / tokens
        wt = w_loc.T
        side = math.isqrt(n // 2)
        me = lax.axis_index("tp")
        x, y = me // 2 % side, me // 2 // side
        order = jnp.array(ORDER, jnp.int32)
        chips = (y + order[:, 1]) % side * side + (x + order[:, 0]) % side
        table = jnp.array([[PLACE[a, b] for b in range(side)] for a in range(side)], jnp.int32)
        every = jnp.arange(side * side, dtype=jnp.int32)
        places = table[(every % side - x) % side, (every // side - y) % side]
        z, xt, m_lane, s_lane = forward(hid_loc, wt, n, 0)
        m_loc = jnp.max(m_lane, axis=1)
        s_loc = jnp.sum(s_lane * jnp.exp(m_lane - m_loc[:, None]), axis=1)
        local = jnp.stack([m_loc.reshape(-1, 2, rows), s_loc.reshape(-1, 2, rows)], axis=2)
        stat = jnp.pad(jnp.take(local, places, axis=0).reshape(n, 2, rows), ((0, 0), (0, 6), (0, 0)))
        mine = jnp.broadcast_to(lab_loc.astype(jnp.float32).reshape(1, rows), (8, rows))
        both = combine(stat, mine, n, 1)
        lse = both[:, 0]
        lab_rel = both[:, 1].astype(jnp.int32) - me * vocab
        in_order = lambda a: jnp.take(a.reshape(n // 2, -1), chips, axis=0).reshape(tokens, 1)
        lse_b = jnp.broadcast_to(in_order(lse + math.log(tokens)), (tokens, LANES))
        lab_b = jnp.broadcast_to(in_order(lab_rel), (tokens, LANES))
        g, dx, t = grad_rows(chips, z, lse_b, lab_b, wt, inv)
        d_hidden = lax.psum_scatter(dx, "tp", scatter_dimension=0, tiled=True)
        d_head = grad_head([xt], [g], vocab).T
        hit_sum = jnp.sum(share(jnp.sum(t.reshape(4, 8, LANES), axis=0), n, 2))
        mean_loss = ((jnp.sum(lse) - hit_sum) * inv).reshape(1)
        return mean_loss, d_hidden.astype(jnp.bfloat16), d_head

    return jax.shard_map(
        local_step,
        mesh=mesh,
        in_specs=(P(("dp", "tp"), None), P(None, "tp"), P(("dp", "tp"))),
        out_specs=(P("dp"), P(("dp", "tp"), None), P("dp", "tp")),
        check_vma=False,
    )
```

time: 493 us -> 452 us (0.917)
  local copies, waits for them, and re-layouts: 51.6 us -> 11 us
  waiting for transfers between devices: 66.1 us -> 50.2 us
  Pallas kernels: 344 us -> 356 us
    pallas_call x2 -> x3, Pallas kernels: 180 us -> 230 us  [the longest x1 123 us: forward(): pl.pallas_call(functools.partial(fwd_kernel, n), name='forward', grid=(to...]
    unnamed x6 -> x12, local copies, waits for them, and re-layouts: 43.5 us -> 0.7 us
    pallas_call x3 -> x1, Pallas kernels: 48.2 us -> 9.97 us  [share(): pl.pallas_call(functools.partial(share_kernel, n), name=f'share{ident}',...]
    all_gather x1 -> x0, waiting for transfers between devices: 33.6 us -> none  [local_step(): hid_all = lax.all_gather(hid_loc, 'tp', axis=0, tiled=True)]
    reduce_scatter x1, waiting for transfers between devices: 31.7 us -> 50.2 us  [local_step(): d_hidden = lax.psum_scatter(dx, 'tp', scatter_dimension=0, tiled=True)]
  transfers between devices with their start and end apart: 2 -> 1, of which waited for: 2 -> 1; matrix products, arithmetic and copies ran while one was open for 10% -> 0% of each run, Pallas kernels for 23% -> 22%
where the time goes in v2:
time: 452 us; the launch traced here: 451 us
  Pallas kernels  356 us (79%)
  waiting for transfers between devices  50.2 us (11%)
  other arithmetic  16.7 us (4%)
  between operations  16.7 us (4%)
  local copies, waits for them, and re-layouts  11 us (2%)
    pallas_call x1, Pallas kernels, forward(): pl.pallas_call(functools.partial(fwd_kernel, n), name='forward', grid=(to...  123 us
    pallas_call x1, Pallas kernels, grad_rows(): pl.pallas_call(functools.partial(grad_kernel, inv), name='grad_rows', gri...  116 us
    pallas_call x1, Pallas kernels, grad_head(): pl.pallas_call(functools.partial(head_kernel, len(xts)), name='grad_head'...  90.6 us
    reduce_scatter x1, waiting for transfers between devices, local_step(): d_hidden = lax.psum_scatter(dx, 'tp', scatter_dimension=0, tiled=True)  50.2 us
    pallas_call x1, Pallas kernels, combine(): pl.pallas_call(functools.partial(combine_kernel, n), name='combine', out_...  16.6 us
    pallas_call x1, Pallas kernels, share(): pl.pallas_call(functools.partial(share_kernel, n), name=f'share{ident}',...  9.97 us
  transfers between devices with their start and end apart: 1, of which 1 were waited for; matrix products, arithmetic and copies ran while one was open for 0% of the time, Pallas kernels for 22%

profile of v2, /device:TPU:97, one launch (start us, length us, event | category | flops | bytes accessed | tf_op | source)
XLA Modules:
  0.0 450.9 jit_solution(10173527435408432761)
XLA Ops:
  7.2 0.1 reduce-scatter.2.cloned.1.call-start
  7.3 1.3 fusion.chips_ref
  8.6 1.2 and_bitcast_fusion
  9.8 1.4 gather_fusion
  11.2 1.2 convert_element_type.13
  12.3 0.1 broadcast_in_dim.50
  12.4 0.6 broadcast_in_dim.51
  13.0 0.6 pad_clamp_fusion
  13.6 0.6 pad_clamp_fusion.1
  14.2 123.1 %forward.1 = (f32[4096,4096]{1,0:T(8,128)}, bf16[2048,4096]{1,0:T(8,128)(2,1)}, f32[4096,128]{1,0:T(8,128)}, f32[4096,128]{1,0:T(8,128)}) custom-call(bf16[128,2048]{1,0:T(8,128)(2,1)} %x_ref.1, bf16[4008,2048]{1,0:T(8,128)(2,1)} %bitcast.57), custom_call_target="tpu_custom_call" | custom-call | flops 68719476736 | bytes 100663296 | tf_op jit(solution)/shard_map/forward/pallas_call | solution.py:373
  137.3 0.0 copy-start
  137.3 2.4 reduce_max.9
  139.7 0.0 copy-done
  139.7 0.0 copy-start.3
  139.7 0.0 copy-start.4
  139.7 0.0 copy-start.2
  139.7 2.5 multiply_reduce_fusion
  142.3 0.7 gather_fusion.1
  143.0 0.0 copy-done.3
  143.0 0.1 bitcast_select_fusion
  143.1 0.7 pad.4.stat_ref
  143.8 0.0 copy-done.4
  143.8 0.6 broadcast_in_dim.54.mine_ref
  144.4 16.6 %combine.1 = f32[32,8,128]{2,1,0:T(8,128)} custom-call(f32[32,8,128]{2,1,0:T(8,128)} %pad.4.stat_ref, f32[8,128]{1,0:T(8,128)} %broadcast_in_dim.54.mine_ref), custom_call_target="tpu_custom_call" | custom-call | tf_op jit(solution)/shard_map/combine/pallas_call | solution.py:120
  161.0 1.6 add_reduce_fusion
  162.5 1.0 subtract_reduce_fusion
  163.5 0.7 gather_fusion.2
  164.2 0.0 copy-done.2
  164.2 0.1 select_bitcast_fusion.1
  164.3 0.7 gather_fusion.3
  165.0 0.1 select_bitcast_fusion
  165.1 3.0 broadcast_in_dim.59.lab_ref
  168.1 1.9 broadcast_in_dim.57.lse_ref
  170.0 115.9 %grad_rows.1 = (bf16[4096,4096]{1,0:T(8,128)(2,1)}, f32[4096,2048]{1,0:T(8,128)}, f32[32,128]{1,0:T(8,128)}) custom-call(s32[16]{0:T(128)} %fusion.chips_ref, f32[4096,4096]{1,0:T(8,128)} %get-tuple-element.12.z_ref, f32[4096,128]{1,0:T(8,128)} %broadcast_in_dim.57.lse_ref, s32[4096,128]{1,0:T(8,128)} %broadcast_in_dim.59.lab_ref, bf16[4008,2048]{1,0:T(8,128)(2,1)} %bitcast.58), custom_call_target="tpu_custom_call" | custom-call | flops 68719476736 | bytes 100663296 | tf_op jit(solution)/shard_map/grad_rows/pallas_call | solution.py:510
  286.0 0.0 copy-start.1
  286.0 0.1 reduce-scatter.2.cloned.1.call-update
  286.1 0.6 copy-done.1
  286.7 0.6 bitcast_reduce_fusion.x_ref
  287.3 10.0 %share2.1 = f32[32,8,128]{2,1,0:T(8,128)} custom-call(f32[8,128]{1,0:T(8,128)} %bitcast_reduce_fusion.x_ref), custom_call_target="tpu_custom_call" | custom-call | tf_op jit(solution)/shard_map/share2/pallas_call | solution.py:65
  297.3 1.5 reduce_sum.39
  300.1 90.6 %grad_head.1 = bf16[4008,2048]{1,0:T(8,128)(2,1)} custom-call(bf16[2048,4096]{1,0:T(8,128)(2,1)} %get-tuple-element.15.refs_0_, bf16[4096,4096]{1,0:T(8,128)(2,1)} %get-tuple-element.16.refs_1_), custom_call_target="tpu_custom_call" | custom-call | flops 68719476736 | bytes 67108864 | tf_op jit(solution)/shard_map/grad_head/pallas_call | solution.py:565
  390.7 50.2 %reduce-scatter.2.cloned.1.call-done = f32[128,2048]{1,0:T(8,128)} async-done(((f32[4096,2048]{1,0:T(8,128)}), f32[128,2048]{1,0:T(8,128)}) %reduce-scatter.2.cloned.1.call-update) | async-done | bytes 1048592 | tf_op jit(solution)/shard_map/reduce_scatter | solution.py:608
  440.9 2.1 convert_element_type.15
  (8 shorter events, 0.1 us)
Async XLA Ops:
  7.2 433.7 %reduce-scatter.2.cloned.1.call-start = ((), (), s32[]{:S(2)}) async-start(), calls=%async_computation.1 | async-start | bytes 34603008 | tf_op jit(solution)/shard_map/reduce_scatter | solution.py:608
  137.3 2.4 copy-start
  139.7 3.3 copy-start.3
  139.7 4.1 copy-start.4
  139.7 24.5 %copy-start.2 = (pred[16]{0:T(512)(128)(4,1)S(1)}, pred[16]{0:T(512)(128)(4,1)}, u32[]{:S(2)}) copy-start(pred[16]{0:T(512)(128)(4,1)} %get-tuple-element.19) | copy-start | bytes 52
  286.0 0.7 copy-start.1
Sparse Core Ops, SparseCore 0:
  286.2 154.6 reduce-scatter.1

commit v3 on v2

--- a/solution.py
+++ b/solution.py
@@ -14,63 +14,6 @@
 CT = 512
 NEG = -3.0e38
 VMEM_LIMIT = 60 * 1024 * 1024
-
-
-def share_kernel(n, x_ref, out_ref, send_sem, recv_sem):
-    me = lax.axis_index("tp")
-    barrier = pltpu.get_barrier_semaphore()
-
-    def greet(k, carry):
-        pl.semaphore_signal(barrier, inc=1, device_id={"tp": lax.rem(me + k, n)}, device_id_type=MESH)
-        return carry
-
-    lax.fori_loop(1, n, greet, 0)
-    pl.semaphore_wait(barrier, n - 1)
-
-    def copy_to(k):
-        peer = lax.rem(me + k, n)
-        return pltpu.make_async_remote_copy(
-            src_ref=x_ref,
-            dst_ref=out_ref.at[me],
-            send_sem=send_sem.at[peer],
-            recv_sem=recv_sem.at[me],
-            device_id={"tp": peer},
-            device_id_type=MESH,
-        )
-
-    def start(k, carry):
-        copy_to(k).start()
-        return carry
-
-    lax.fori_loop(1, n, start, 0)
-    out_ref[me] = x_ref[...]
-
-    def finish(k, carry):
-        peer = lax.rem(me + k, n)
-        copy_to(k).wait_send()
-        pltpu.make_async_remote_copy(
-            src_ref=x_ref,
-            dst_ref=out_ref.at[peer],
-            send_sem=send_sem.at[peer],
-            recv_sem=recv_sem.at[peer],
-            device_id={"tp": peer},
-            device_id_type=MESH,
-        ).wait_recv()
-        return carry
-
-    lax.fori_loop(1, n, finish, 0)
-
-
-def share(x, n, ident):
-    return pl.pallas_call(
-        functools.partial(share_kernel, n),
-        name=f"share{ident}",
-        out_shape=jax.ShapeDtypeStruct((n, *x.shape), x.dtype),
-        in_specs=[pl.BlockSpec(memory_space=pltpu.VMEM)],
-        out_specs=pl.BlockSpec(memory_space=pltpu.VMEM),
-        scratch_shapes=[pltpu.SemaphoreType.DMA((n,)), pltpu.SemaphoreType.DMA((n,))],
-        compiler_params=pltpu.CompilerParams(collective_id=ident, has_side_effects=True),
-    )(x)
 
 
 def combine_kernel(n, stat_ref, mine_ref, out_ref, got, row, send_a, recv_a, send_b, recv_b):
@@ -409,34 +352,98 @@
     )(x, wt)
 
 
-def grad_kernel(inv, chips_ref, z_ref, lse_ref, lab_ref, wt_hbm, g_ref, dx_hbm, t_ref, w_scr, g0, g1, dx0, dx1, sem, out_sem):
+def grad_kernel(
+    n, inv, z_ref, lse_ref, lab_ref, wt_hbm, g_hbm, sum_hbm, hit_ref,
+    t_ref, hits, hit_send, hit_recv, w_scr, g0, g1, dx0, dx1, pr0, pr1, sem, g_sem, out_sem, send_sem, recv_sem, free_sem,
+):
+    side = math.isqrt(n // 2)
     padded, hidden = w_scr.shape
     vocab = wt_hbm.shape[0]
     step = pl.program_id(0)
     steps = pl.num_programs(0)
     pieces = padded // CT
     width = hidden // pieces
+    rows = TT // 4
     lane = lax.broadcasted_iota(jnp.int32, (32, LANES), 1)
+    me = lax.axis_index("tp")
+    core = lax.rem(me, 2)
+    partner = me + 1 - 2 * core
+    chip = me // 2
+    x, y = lax.rem(chip, side), chip // side
+
+    def each(body):
+        def peers(k, carry):
+            body(lax.rem(me + k, n))
+            return carry
+
+        lax.fori_loop(1, n, peers, 0)
+
+    def tell(peer, slot):
+        return pltpu.make_async_remote_copy(
+            src_ref=t_ref.at[pl.ds(0, 8), :],
+            dst_ref=hits.at[slot],
+            send_sem=hit_send.at[peer],
+            recv_sem=hit_recv.at[slot],
+            device_id={"tp": peer},
+            device_id_type=MESH,
+        )
+
+    def chip_at(place):
+        dx = dy = 0
+        for k, (ax, ay) in enumerate(ORDER):
+            dx = dx + jnp.where(place == k, ax, 0)
+            dy = dy + jnp.where(place == k, ay, 0)
+        return lax.rem(y + dy, side) * side + lax.rem(x + dx, side)
 
     def probs(j, g):
         for r in range(0, TT, 32):
-            rows = pl.ds(r, 32)
-            lse = lse_ref[rows, :]
-            rel = lab_ref[rows, :] - j * CT
+            part = pl.ds(r, 32)
+            lse = lse_ref[part, :]
+            rel = lab_ref[part, :] - j * CT
             t = t_ref[...]
             for k in range(CT // LANES):
                 at = pl.ds(pl.multiple_of(j * CT + k * LANES, LANES), LANES)
-                z = z_ref[rows, at]
+                z = z_ref[part, at]
                 p = jnp.exp(z - lse)
                 hit = rel == lane + k * LANES
                 t = t + jnp.where(hit, z, 0.0)
-                gv = jnp.where(hit, p - inv, p).astype(jnp.bfloat16)
-                g[rows, at] = gv
-                g_ref[rows, at] = gv
+                g[part, at] = jnp.where(hit, p - inv, p).astype(jnp.bfloat16)
             t_ref[...] = t
+
+    def g_copy(tile, par, g):
+        return pltpu.make_async_copy(g, g_hbm.at[pl.ds(pl.multiple_of(tile * TT, TT), TT), :], g_sem.at[par])
+
+    def own(dx, k):
+        return dx.at[pl.ds(pl.multiple_of(2 * k * rows + core * rows, rows), rows), :]
+
+    def trade(par, dx, pr, k):
+        return pltpu.make_async_remote_copy(
+            src_ref=dx.at[pl.ds(pl.multiple_of(2 * k * rows + (1 - core) * rows, rows), rows), :],
+            dst_ref=pr.at[k],
+            send_sem=send_sem.at[par, k],
+            recv_sem=recv_sem.at[par, k],
+            device_id={"tp": partner},
+            device_id_type=MESH,
+        )
+
+    def leave(tile, par, dx, k):
+        return pltpu.make_async_copy(own(dx, k), sum_hbm.at[chip_at(tile * 2 + k)], out_sem.at[par, k])
+
+    def merge(tile, par, dx, pr):
+        for k in range(2):
+            trade(par, dx, pr, k).wait()
+            at = pl.ds(pl.multiple_of(2 * k * rows + core * rows, rows), rows)
+            dx[at, :] = dx[at, :] + pr[k]
+            leave(tile, par, dx, k).start()
+
+        @pl.when(tile + 2 < steps - 1)
+        def _():
+            pl.semaphore_signal(free_sem.at[par], inc=1, device_id={"tp": partner}, device_id_type=MESH)
 
     @pl.when(step == 0)
     def _():
+        barrier = pltpu.get_barrier_semaphore()
+        each(lambda peer: pl.semaphore_signal(barrier, inc=1, device_id={"tp": peer}, device_id_type=MESH))
         load = pltpu.make_async_copy(wt_hbm, w_scr.at[pl.ds(0, vocab), :], sem)
         load.start()
         w_scr[pl.ds(vocab, padded - vocab), :] = jnp.zeros((padded - vocab, hidden), jnp.bfloat16)
@@ -447,34 +454,28 @@
             return carry
 
         lax.fori_loop(0, pieces, piece, 0)
+        g_copy(0, 0, g0).start()
         load.wait()
-
-    per_chip = TT // 2
-
-    def leave(at, dx):
-        return [
-            pltpu.make_async_copy(
-                dx.at[pl.ds(k * per_chip, per_chip), :],
-                dx_hbm.at[pl.ds(pl.multiple_of(chips_ref[at * 2 + k] * per_chip, per_chip), per_chip), :],
-                out_sem.at[lax.rem(at, 2), k],
-            )
-            for k in range(2)
-        ]
+        pl.semaphore_wait(barrier, n - 1)
 
     def back(j, g, dx):
         at = pl.ds(pl.multiple_of(j * width, width), width)
         dx[:, at] = jnp.dot(g[...], w_scr[:, at], preferred_element_type=jnp.float32)
 
-    for parity, (now, later, dx) in enumerate(((g1, g0, dx1), (g0, g1, dx0))):
-
-        @pl.when((step > 2) & (lax.rem(step, 2) == parity))
-        def _(dx=dx):
-            for c in leave(step - 3, dx):
-                c.wait()
+    buffers = ((dx0, pr0), (dx1, pr1))
+    for parity, (now, later) in enumerate(((g1, g0), (g0, g1))):
+        dx, pr = buffers[1 - parity]
+        old = buffers[parity]
+
+        def halfway(j, parity=parity, old=old):
+            @pl.when((j == pieces // 2) & (step > 1))
+            def _():
+                merge(step - 2, parity, *old)
 
         @pl.when((step > 0) & (step < steps - 1) & (lax.rem(step, 2) == parity))
-        def _(now=now, later=later, dx=dx):
+        def _(now=now, later=later, dx=dx, halfway=halfway):
             def piece(j, carry):
+                halfway(j)
                 back(j, now, dx)
                 probs(j, later)
                 return carry
@@ -484,62 +485,92 @@
         if parity == 0:
 
             @pl.when(step == steps - 1)
-            def _(now=now, dx=dx):
+            def _(now=now, dx=dx, halfway=halfway):
+                mine = t_ref[0:8, :] + t_ref[8:16, :] + t_ref[16:24, :] + t_ref[24:32, :]
+                t_ref[0:8, :] = mine
+                hits[me] = mine
+                each(lambda peer: tell(peer, me).start())
+
                 def piece(j, carry):
+                    halfway(j)
                     back(j, now, dx)
                     return carry
 
                 lax.fori_loop(0, pieces, piece, 0)
 
+        @pl.when((step > 1) & (lax.rem(step, 2) == parity))
+        def _(parity=parity, old=old):
+            for k in range(2):
+                leave(step - 2, parity, old[0], k).wait()
+
         @pl.when((step > 0) & (lax.rem(step, 2) == parity))
-        def _(dx=dx):
-            for c in leave(step - 1, dx):
-                c.start()
+        def _(parity=parity, now=now, dx=dx, pr=pr):
+            @pl.when(step > 2)
+            def _():
+                pl.semaphore_wait(free_sem.at[1 - parity], 1)
+
+            for k in range(2):
+                trade(1 - parity, dx, pr, k).start()
+            g_copy(step - 1, 1 - parity, now).wait()
+
+        @pl.when((step > 0) & (step < steps - 1) & (lax.rem(step, 2) == parity))
+        def _(parity=parity, later=later):
+            g_copy(step, parity, later).start()
 
     @pl.when(step == steps - 1)
     def _():
-        for c in leave(step - 2, dx0) + leave(step - 1, dx1):
-            c.wait()
-
-
-def grad_rows(chips, z, lse, lab, wt, inv):
+        merge(step - 1, 1, dx1, pr1)
+        each(lambda peer: tell(peer, peer).wait_recv())
+        each(lambda peer: tell(peer, me).wait_send())
+        hit_ref[...] = hits[...]
+        for k in range(2):
+            leave(step - 1, 1, dx1, k).wait()
+
+
+def grad_rows(z, lse, lab, wt, n, inv, ident):
     tokens, padded = z.shape
     hidden = wt.shape[1]
     steps = tokens // TT
     ahead = lambda i: (jnp.minimum(i, steps - 1), 0)
+    any_spec = pl.BlockSpec(memory_space=pl.ANY)
     return pl.pallas_call(
-        functools.partial(grad_kernel, inv),
+        functools.partial(grad_kernel, n, inv),
         name="grad_rows",
         grid=(steps + 1,),
         out_shape=(
             jax.ShapeDtypeStruct((tokens, padded), jnp.bfloat16),
-            jax.ShapeDtypeStruct((tokens, hidden), jnp.float32),
-            jax.ShapeDtypeStruct((32, LANES), jnp.float32),
+            jax.ShapeDtypeStruct((n // 2, tokens // n, hidden), jnp.float32),
+            jax.ShapeDtypeStruct((n, 8, LANES), jnp.float32),
         ),
         in_specs=[
-            pl.BlockSpec(memory_space=pltpu.SMEM),
             pl.BlockSpec((TT, padded), ahead),
             pl.BlockSpec((TT, LANES), ahead),
             pl.BlockSpec((TT, LANES), ahead),
-            pl.BlockSpec(memory_space=pl.ANY),
+            any_spec,
         ],
-        out_specs=(
-            pl.BlockSpec((TT, padded), ahead),
-            pl.BlockSpec(memory_space=pl.ANY),
-            pl.BlockSpec((32, LANES), lambda i: (0, 0)),
-        ),
+        out_specs=(any_spec, any_spec, pl.BlockSpec((n, 8, LANES), lambda i: (0, 0, 0))),
         scratch_shapes=[
+            pltpu.VMEM((32, LANES), jnp.float32),
+            pltpu.VMEM((n, 8, LANES), jnp.float32),
+            pltpu.SemaphoreType.DMA((n,)),
+            pltpu.SemaphoreType.DMA((n,)),
             pltpu.VMEM((padded, hidden), jnp.bfloat16),
             pltpu.VMEM((TT, padded), jnp.bfloat16),
             pltpu.VMEM((TT, padded), jnp.bfloat16),
             pltpu.VMEM((TT, hidden), jnp.float32),
             pltpu.VMEM((TT, hidden), jnp.float32),
+            pltpu.VMEM((2, TT // 4, hidden), jnp.float32),
+            pltpu.VMEM((2, TT // 4, hidden), jnp.float32),
             pltpu.SemaphoreType.DMA,
+            pltpu.SemaphoreType.DMA((2,)),
             pltpu.SemaphoreType.DMA((2, 2)),
+            pltpu.SemaphoreType.DMA((2, 2)),
+            pltpu.SemaphoreType.DMA((2, 2)),
+            pltpu.SemaphoreType.REGULAR((2,)),
         ],
-        compiler_params=pltpu.CompilerParams(vmem_limit_bytes=VMEM_LIMIT),
+        compiler_params=pltpu.CompilerParams(vmem_limit_bytes=67_043_328, collective_id=ident, has_side_effects=True),
         cost_estimate=pl.CostEstimate(flops=2 * tokens * hidden * padded, bytes_accessed=6 * tokens * padded, transcendentals=0),
-    )(chips, z, lse, lab, wt)
+    )(z, lse, lab, wt)
 
 
 def head_kernel(parts, *refs):
@@ -604,10 +635,13 @@
         in_order = lambda a: jnp.take(a.reshape(n // 2, -1), chips, axis=0).reshape(tokens, 1)
         lse_b = jnp.broadcast_to(in_order(lse + math.log(tokens)), (tokens, LANES))
         lab_b = jnp.broadcast_to(in_order(lab_rel), (tokens, LANES))
-        g, dx, t = grad_rows(chips, z, lse_b, lab_b, wt, inv)
-        d_hidden = lax.psum_scatter(dx, "tp", scatter_dimension=0, tiled=True)
+        g, dx, t = grad_rows(z, lse_b, lab_b, wt, n, inv, 3)
+        same_core = [list(range(k, n, 2)) for k in range(2)]
+        d_hidden = lax.psum_scatter(
+            dx.reshape(tokens // 2, hidden), "tp", scatter_dimension=0, axis_index_groups=same_core, tiled=True
+        )
         d_head = grad_head([xt], [g], vocab).T
-        hit_sum = jnp.sum(share(jnp.sum(t.reshape(4, 8, LANES), axis=0), n, 2))
+        hit_sum = jnp.sum(t)
         mean_loss = ((jnp.sum(lse) - hit_sum) * inv).reshape(1)
         return mean_loss, d_hidden.astype(jnp.bfloat16), d_head
 

time: 452 us -> 401 us (0.89)
  waiting for transfers between devices: 50.2 us -> 10 us
  Pallas kernels: 356 us -> 348 us
    reduce_scatter x1, waiting for transfers between devices: 50.2 us -> 9.97 us  [local_step(): lax.psum_scatter(dx.reshape(tokens // 2, hidden), 'tp', scatter_dimension...]
    pallas_call x2 -> x1, Pallas kernels: 126 us -> 118 us  [grad_rows(): pl.pallas_call(functools.partial(grad_kernel, n, inv), name='grad_rows',...]
  transfers between devices with their start and end apart: 1 -> 1, of which waited for: 1 -> 1; matrix products, arithmetic and copies ran while one was open for 0% -> 0% of each run, Pallas kernels for 22% -> 23%
where the time goes in v3:
time: 401 us; the launch traced here: 400 us
  Pallas kernels  348 us (87%)
  between operations  16.7 us (4%)
  other arithmetic  14 us (3%)
  local copies, waits for them, and re-layouts  11.2 us (3%)
  waiting for transfers between devices  10 us (2%)
    pallas_call x1, Pallas kernels, forward(): pl.pallas_call(functools.partial(fwd_kernel, n), name='forward', grid=(to...  123 us
    pallas_call x1, Pallas kernels, grad_rows(): pl.pallas_call(functools.partial(grad_kernel, n, inv), name='grad_rows',...  118 us
    pallas_call x1, Pallas kernels, grad_head(): pl.pallas_call(functools.partial(head_kernel, len(xts)), name='grad_head'...  90.6 us
    pallas_call x1, Pallas kernels, combine(): pl.pallas_call(functools.partial(combine_kernel, n), name='combine', out_...  16.5 us
    reduce_scatter x1, waiting for transfers between devices, local_step(): lax.psum_scatter(dx.reshape(tokens // 2, hidden), 'tp', scatter_dimension...  9.97 us
  transfers between devices with their start and end apart: 1, of which 1 were waited for; matrix products, arithmetic and copies ran while one was open for 0% of the time, Pallas kernels for 23%

profile of v3, /device:TPU:97, one launch (start us, length us, event | category | flops | bytes accessed | tf_op | source)
XLA Modules:
  0.0 400.0 jit_solution(10353992577823683795)
XLA Ops:
  7.2 0.1 reduce-scatter.2.cloned.1.call-start
  7.3 1.4 gather_fusion
  8.7 1.2 convert_element_type.13
  9.9 0.1 broadcast_in_dim.50
  9.9 0.6 broadcast_in_dim.51
  10.6 1.2 and_bitcast_fusion
  11.8 0.6 pad_clamp_fusion
  12.4 0.6 pad_clamp_fusion.1
  13.0 123.1 %forward.1 = (f32[4096,4096]{1,0:T(8,128)}, bf16[2048,4096]{1,0:T(8,128)(2,1)}, f32[4096,128]{1,0:T(8,128)}, f32[4096,128]{1,0:T(8,128)}) custom-call(bf16[128,2048]{1,0:T(8,128)(2,1)} %x_ref.1, bf16[4008,2048]{1,0:T(8,128)(2,1)} %bitcast.29), custom_call_target="tpu_custom_call" | custom-call | flops 68719476736 | bytes 100663296 | tf_op jit(solution)/shard_map/forward/pallas_call | solution.py:316
  136.1 0.0 copy-start
  136.1 2.4 reduce_max.9
  138.5 0.0 copy-done
  138.5 0.0 copy-start.3
  138.5 0.0 copy-start.4
  138.5 0.0 copy-start.2
  138.5 2.5 multiply_reduce_fusion
  141.1 0.7 gather_fusion.1
  141.8 0.0 copy-done.3
  141.8 0.1 bitcast_select_fusion
  141.9 0.7 pad.4.stat_ref
  142.6 0.0 copy-done.4
  142.6 0.6 broadcast_in_dim.54.mine_ref
  143.2 16.5 %combine.1 = f32[32,8,128]{2,1,0:T(8,128)} custom-call(f32[32,8,128]{2,1,0:T(8,128)} %pad.4.stat_ref, f32[8,128]{1,0:T(8,128)} %broadcast_in_dim.54.mine_ref), custom_call_target="tpu_custom_call" | custom-call | tf_op jit(solution)/shard_map/combine/pallas_call | solution.py:63
  159.7 1.6 add_reduce_fusion
  161.3 1.0 subtract_reduce_fusion
  162.2 0.7 gather_fusion.2
  162.9 0.0 copy-done.2
  163.0 0.1 select_bitcast_fusion.1
  163.1 0.7 gather_fusion.3
  163.8 0.1 select_bitcast_fusion
  163.8 3.0 broadcast_in_dim.59.lab_ref
  166.8 1.9 broadcast_in_dim.57.lse_ref
  168.7 117.8 %grad_rows.1 = (bf16[4096,4096]{1,0:T(8,128)(2,1)}, f32[16,128,2048]{2,1,0:T(8,128)}, f32[32,8,128]{2,1,0:T(8,128)}) custom-call(f32[4096,4096]{1,0:T(8,128)} %get-tuple-element.12.z_ref, f32[4096,128]{1,0:T(8,128)} %broadcast_in_dim.57.lse_ref, s32[4096,128]{1,0:T(8,128)} %broadcast_in_dim.59.lab_ref, bf16[4008,2048]{1,0:T(8,128)(2,1)} %bitcast.30), custom_call_target="tpu_custom_call" | custom-call | flops 68719476736 | bytes 100663296 | tf_op jit(solution)/shard_map/grad_rows/pallas_call | solution.py:536
  286.6 0.0 copy-start.1
  286.6 0.1 reduce-scatter.2.cloned.1.call-update
  286.6 0.8 copy-done.1
  287.5 0.6 reduce_sum.29
  289.4 90.6 %grad_head.1 = bf16[4008,2048]{1,0:T(8,128)(2,1)} custom-call(bf16[2048,4096]{1,0:T(8,128)(2,1)} %get-tuple-element.15.refs_0_, bf16[4096,4096]{1,0:T(8,128)(2,1)} %get-tuple-element.16.refs_1_), custom_call_target="tpu_custom_call" | custom-call | flops 68719476736 | bytes 67108864 | tf_op jit(solution)/shard_map/grad_head/pallas_call | solution.py:596
  380.0 10.0 %reduce-scatter.2.cloned.1.call-done = f32[128,2048]{1,0:T(8,128)} async-done(((f32[2048,2048]{1,0:T(8,128)}), f32[128,2048]{1,0:T(8,128)}) %reduce-scatter.2.cloned.1.call-update) | async-done | bytes 1048592 | tf_op jit(solution)/shard_map/reduce_scatter | solution.py:640
  390.0 2.1 convert_element_type.15
  (8 shorter events, 0.1 us)
Async XLA Ops:
  7.2 382.8 %reduce-scatter.2.cloned.1.call-start = ((), (), s32[]{:S(2)}) async-start(), calls=%async_computation.1 | async-start | bytes 17825792 | tf_op jit(solution)/shard_map/reduce_scatter | solution.py:640
  136.1 2.4 copy-start
  138.5 3.3 copy-start.3
  138.5 4.1 %copy-start.4 = (f32[128]{0:T(128)S(1)}, f32[128]{0:T(128)}, u32[]{:S(2)}) copy-start(f32[128]{0:T(128)} %convert_element_type.13) | copy-start | bytes 1540
  138.5 24.4 %copy-start.2 = (pred[16]{0:T(512)(128)(4,1)S(1)}, pred[16]{0:T(512)(128)(4,1)}, u32[]{:S(2)}) copy-start(pred[16]{0:T(512)(128)(4,1)} %get-tuple-element.19) | copy-start | bytes 52
  286.6 0.9 copy-start.1
Sparse Core Ops, SparseCore 0:
  286.8 103.1 reduce-scatter.1
